TPU v7x, 32 devices: a whole 2x2x4 slice. The times are simulated.
32 devices in a mesh: gx: 8 (over y, x, core), gy: 4 (over z).
Axes of the slice: x: 2, y: 2, z: 4, core: 2. Of those that a mesh axis runs over, the one named last changes fastest.
Arguments:
- source_field: bfloat16 [4096, 128, 128], P(('gx', 'gy')), may hold values from -6 to 6
- weight_blocks: bfloat16 [16384, 128, 128], P(('gx', 'gy')), may hold values from -0.1875 to 0.1875
- source_ids: int32 [16384], replicated, may hold values from 0 to 4095, as said below
- target_ids: int32 [16384], replicated, may hold values from 0 to 2047, as said below
Outputs:
- remapped: bfloat16 [2048, 128, 128], P(('gx', 'gy'))
Inputs may be any that keep to these rules, and one draw needn't show every extreme that they name: `source_ids`: source block b lies on device b // 128 of gx+gy, and weight block k lies on device k // 512. The weight blocks of device d name only source blocks of devices d - 2 to d + 2. Among the weight blocks of one device, at most 64 distinct source blocks of any one other device are named, and exactly 64 for some other device. `target_ids`: target block t lies on device t // 64 of gx+gy. The weight blocks of device d name only target blocks of devices d - 2 to d + 2. Among the weight blocks of one device, at most 16 distinct target blocks of any one device are named, and exactly 16 for some other device.
All inputs are finite; a program needn't handle non-finite values.
Results may differ from a plain program's by a relative error of at most 0.001.
Values may be sent and summed in bfloat16 or wider, within the bound.
A program may use at most 192 MiB of HBM per device.

v0:
```python
import functools

import jax
import jax.numpy as jnp
from jax import lax
from jax.experimental import pallas as pl
from jax.experimental.pallas import tpu as pltpu
from jax.sharding import PartitionSpec as P


HALF = 2
TB_DEV = 64
CAP_S = 64
CAP_T = 16
SPAN = 2 * HALF + 1
AXES = ("gx", "gy")
MESH = pl.DeviceIdType.MESH
QUAD = 4
CHUNK = 4
GROUP = 8
TILE = 128
RARE = 12
LOW_EXPONENT = -110.0


def passed_along(value, steps):
    count = lax.axis_size(AXES)
    initial, last = (max(0, -steps), min(count, count - steps))
    return lax.ppermute(value, AXES, [(source, source + steps) for source in range(initial, last)])


def rows_of(ids, device, devices, held):
    clamped = jnp.clip(device, 0, devices - 1)
    return lax.dynamic_slice_in_dim(ids, clamped * held, held, 0)


def named(rows, low, count):
    return jnp.any(rows[:, None] == low + jnp.arange(count, dtype=jnp.int32)[None, :], axis=0)


def ranks_of(asked):
    count = asked.shape[1]
    before = jnp.arange(count)[:, None] < jnp.arange(count)[None, :]
    return jnp.sum((asked[:, :, None] & before[None]).astype(jnp.int32), axis=1)


def exchange_kernel(devices, n_gy, count, sel, src, recv, srcv, hst, xst, lsem, rsem, ssem):
    nb = src.shape[0]
    pieces = count // CHUNK
    half = CAP_S // CHUNK
    me = lax.axis_index("gx") * n_gy + lax.axis_index("gy")
    r = lax.rem(me, QUAD)
    inner = (r == 1) | (r == 2)
    outer = jnp.logical_not(inner)
    sgn = jnp.where(r < 2, 1, -1)
    partner = me + 1 - 2 * lax.rem(r, 2)
    near = me + sgn
    far = me + 2 * sgn
    to = me + QUAD * sgn
    source = me - QUAD * sgn
    has_to = (to >= 0) & (to < devices)
    has_from = (source >= 0) & (source < devices)
    base_a, base_b, base_c, base_h, base_o = 0, nb, 2 * nb, 3 * nb, 3 * nb + CAP_S

    def at(device):
        return (device // n_gy, lax.rem(device, n_gy))

    barrier = pltpu.get_barrier_semaphore()

    def greet(device):
        pl.semaphore_signal(barrier, inc=1, device_id=at(device), device_id_type=MESH)

    greet(partner)
    greet(far)
    pl.when(inner)(lambda: greet(near))
    pl.when(has_to)(lambda: greet(to))
    pl.when(has_from)(lambda: greet(source))
    peers = 2 + inner.astype(jnp.int32) + has_to.astype(jnp.int32) + has_from.astype(jnp.int32)
    pl.semaphore_wait(barrier, peers)

    def piece(base, k):
        return recv.at[pl.ds(base + k * CHUNK, CHUNK)]

    def copy(ref, base, k, send, got, device):
        return pltpu.make_async_remote_copy(
            src_ref=ref,
            dst_ref=piece(base, k),
            send_sem=ssem.at[send, k],
            recv_sem=rsem.at[got, k],
            device_id=at(device),
            device_id_type=MESH,
        )

    def cross_inner(k):
        return copy(xst.at[pl.ds(k * CHUNK, CHUNK)], base_a, k, 0, 0, near)

    def cross_outer(k):
        return copy(xst.at[pl.ds(k * CHUNK, CHUNK)], base_b, k, 0, 1, far)

    def side(k):
        return copy(hst.at[pl.ds(k * CHUNK, CHUNK)], base_h, k, 1, 3, partner)

    def ahead(k):
        return copy(piece(base_a, k), base_a, k, 2, 0, partner)

    def over_outer(k):
        return copy(piece(base_a, k), base_b, k, 3, 1, to)

    def over_inner(k):
        return copy(piece(base_b, k), base_c, k, 3, 2, to)

    def last(k):
        return copy(piece(base_c, k), base_c, k, 4, 2, partner)

    def await_piece(base, got, k):
        copy(piece(base, k), base, k, 0, got, partner).wait_recv()

    load = pltpu.make_async_copy(src, srcv, lsem.at[0])
    load.start()
    keep = pltpu.make_async_copy(src, recv.at[pl.ds(base_o, nb)], lsem.at[1])
    load.wait()

    def pick(j, carry):
        for u in range(CHUNK):
            xst[j * CHUNK + u] = srcv[sel[CAP_S + j * CHUNK + u]]
        return carry

    def pick_side(j, carry):
        for u in range(CHUNK):
            hst[j * CHUNK + u] = srcv[sel[j * CHUNK + u]]
        return carry

    lax.fori_loop(0, pieces, pick, 0)
    lax.fori_loop(0, half, pick_side, 0)

    @pl.when(inner)
    def _():
        for k in range(pieces):
            cross_inner(k).start()
        for k in range(half):
            side(k).start()

    keep.start()

    @pl.when(outer)
    def _():
        for k in range(pieces):
            cross_outer(k).start()
        for k in range(half):
            side(k).start()
        for k in range(pieces):
            await_piece(base_a, 0, k)

            @pl.when(has_to)
            def _():
                over_outer(k).start()

        @pl.when(has_from)
        def _():
            for k in range(pieces):
                await_piece(base_b, 1, k)
            for k in range(half):
                await_piece(base_c, 2, k)

        for k in range(pieces):
            cross_outer(k).wait_send()

        @pl.when(has_to)
        def _():
            for k in range(pieces):
                over_outer(k).wait_send()

    @pl.when(inner)
    def _():
        def from_far(k):
            await_piece(base_b, 1, k)

            @pl.when(has_to)
            def _():
                over_inner(k).start()

        def from_shift(k):
            if 0 <= k < half:

                @pl.when(has_from)
                def _():
                    await_piece(base_c, 2, k)
                    last(k).start()

        for k in range(pieces):
            from_far(k)
            from_shift(k - 1)
        for k in range(pieces):
            await_piece(base_a, 0, k)
            ahead(k).start()

        @pl.when(has_from)
        def _():
            for k in range(half, pieces):
                await_piece(base_c, 2, k)
            for k in range(half):
                last(k).wait_send()

        for k in range(pieces):
            cross_inner(k).wait_send()
            ahead(k).wait_send()

        @pl.when(has_to)
        def _():
            for k in range(pieces):
                over_inner(k).wait_send()

    for k in range(half):
        await_piece(base_h, 3, k)
        side(k).wait_send()
    keep.wait()


def exchange_call(n_gy, devices, rare, sel, source_field):
    nb = source_field.shape[0]
    tile = source_field.shape[1:]
    kind = source_field.dtype
    count = nb if rare else nb - RARE
    pieces = count // CHUNK
    anywhere = pl.BlockSpec(memory_space=pl.ANY)
    vmem = pl.BlockSpec(memory_space=pltpu.VMEM)
    return pl.pallas_call(
        functools.partial(exchange_kernel, devices, n_gy, count),
        out_shape=jax.ShapeDtypeStruct((4 * nb + CAP_S,) + tile, kind),
        in_specs=[pl.BlockSpec(memory_space=pltpu.SMEM), anywhere],
        out_specs=anywhere if rare else vmem,
        scratch_shapes=[
            pltpu.VMEM((nb,) + tile, kind),
            pltpu.VMEM((CAP_S,) + tile, kind),
            pltpu.VMEM((count,) + tile, kind),
            pltpu.SemaphoreType.DMA((3,)),
            pltpu.SemaphoreType.DMA((4, pieces)),
            pltpu.SemaphoreType.DMA((5, pieces)),
        ],
        name="exchange_all" if rare else "exchange",
        cost_estimate=pl.CostEstimate(flops=2 * 10**10, bytes_accessed=8 * 2**20, transcendentals=0),
        compiler_params=pltpu.CompilerParams(
            collective_id=int(rare), has_side_effects=True, vmem_limit_bytes=12 * 2**20
        ),
    )(sel, source_field)


def products_kernel(groups, bounds, packed, weights, pool, *refs):
    outs, acc = refs[:-1], refs[-1]
    rows = lax.broadcasted_iota(jnp.int32, (CAP_T, TILE), 0)
    for group in groups:
        first = bounds[group]
        rounds = (bounds[group + 1] - first) // GROUP
        acc[...] = jnp.zeros_like(acc)

        def run(g, carry, first=first):
            items = [packed[first + g * GROUP + u] for u in range(GROUP)]
            sums = []
            for item in items:
                k, s = lax.shift_right_logical(item, 16), lax.shift_right_logical(item, 6) & 1023
                sums.append(jnp.dot(weights[k], pool[s], preferred_element_type=jnp.float32))
            for item, value in zip(items, sums):
                acc[item & 63] += value
            return carry

        lax.fori_loop(0, rounds, run, 0)

        if group == HALF:
            outs[0][...] = acc[1 : 1 + CAP_T]
            continue
        for r in range(2):

            def encode(b, exponents, r=r, out=outs[r]):
                value = acc[1 + r * CAP_T + b]
                most = jnp.max(jnp.abs(value), axis=0, keepdims=True)
                exponent = jnp.ceil(jnp.log(jnp.maximum(most, 1e-37)) * 1.4426950408889634)
                exponent = jnp.maximum(exponent, LOW_EXPONENT)
                scaled = jnp.floor(value * jnp.exp2(15.0 - exponent) + 0.5)
                scaled = jnp.clip(scaled, -32767.0, 32767.0)
                out[pl.ds(pl.multiple_of(b * TILE, TILE), TILE), :] = scaled.astype(jnp.int32).astype(jnp.int16)
                return jnp.where(rows == b, exponent.astype(jnp.int32), exponents)

            exponents = lax.fori_loop(0, CAP_T, encode, jnp.zeros((CAP_T, TILE), jnp.int32))
            outs[r][CAP_T * TILE :, :] = exponents.astype(jnp.int16)
        outs = outs[2:]


def products_call(groups, rare, held, bounds, packed, weights, pool):
    tile = pool.shape[1:]
    smem = pl.BlockSpec(memory_space=pltpu.SMEM)
    vmem = pl.BlockSpec(memory_space=pltpu.VMEM)
    out_shape = []
    for group in groups:
        if group == HALF:
            out_shape += [jax.ShapeDtypeStruct((CAP_T,) + tile, jnp.float32)]
        else:
            out_shape += [jax.ShapeDtypeStruct((CAP_T * tile[0] + CAP_T, tile[1]), jnp.int16)] * 2
    share = held * len(groups) // 3
    return pl.pallas_call(
        functools.partial(products_kernel, groups),
        out_shape=out_shape,
        in_specs=[smem, smem, vmem, vmem],
        out_specs=[vmem] * len(out_shape),
        scratch_shapes=[pltpu.VMEM((1 + 2 * CAP_T,) + tile, jnp.float32)],
        cost_estimate=pl.CostEstimate(
            flops=share * 2 * 128**3, bytes_accessed=8 * 2**20, transcendentals=0
        ),
        compiler_params=pltpu.CompilerParams(vmem_limit_bytes=(48 if rare else 24) * 2**20),
    )(bounds, packed, weights, pool)


def final_kernel(targets, *refs):
    boxes, out, acc, scales = refs[:SPAN], refs[SPAN], refs[SPAN + 1], refs[SPAN + 2]
    acc[...] = jnp.zeros_like(acc)
    for s in range(SPAN):
        if s != HALF:
            scales[s] = jnp.exp2(boxes[s][CAP_T * TILE :, :].astype(jnp.float32) - 15.0)

    def one(b, carry):
        for s in range(SPAN):
            if s == HALF:
                value = boxes[s][b]
            else:
                rows = pl.ds(pl.multiple_of(b * TILE, TILE), TILE)
                value = boxes[s][rows, :].astype(jnp.float32) * scales[s, pl.ds(b, 1), :]
            acc[targets[s * CAP_T + b]] += value
        return carry

    lax.fori_loop(0, CAP_T, one, 0)

    def close(g, carry):
        for u in range(GROUP):
            out[g * GROUP + u] = acc[1 + g * GROUP + u].astype(out.dtype)
        return carry

    lax.fori_loop(0, TB_DEV // GROUP, close, 0)


def final_call(targets, boxes):
    tile = boxes[HALF].shape[1:]
    vmem = pl.BlockSpec(memory_space=pltpu.VMEM)
    return pl.pallas_call(
        final_kernel,
        out_shape=jax.ShapeDtypeStruct((TB_DEV,) + tile, jnp.bfloat16),
        in_specs=[pl.BlockSpec(memory_space=pltpu.SMEM)] + [vmem] * SPAN,
        out_specs=vmem,
        scratch_shapes=[
            pltpu.VMEM((1 + TB_DEV,) + tile, jnp.float32),
            pltpu.VMEM((SPAN, CAP_T, tile[1]), jnp.float32),
        ],
        name="final_sum",
        compiler_params=pltpu.CompilerParams(vmem_limit_bytes=16 * 2**20),
    )(targets, *boxes)


def named_blocks(ids, first, nb):
    rel = ids - (first - HALF) * nb
    high, low = rel // nb, rel % nb
    high = high[:, None, :] == jnp.arange(SPAN, dtype=jnp.int32)[None, :, None]
    low = low[:, :, None] == jnp.arange(nb, dtype=jnp.int32)[None, None, :]
    counts = lax.dot_general(
        high.astype(jnp.bfloat16),
        low.astype(jnp.bfloat16),
        (((2,), (1,)), ((0,), (0,))),
        preferred_element_type=jnp.float32,
    )
    return counts > 0.5


def wanted(every, role):
    owners = every.shape[0] - 2 * HALF

    def asked_from(step):
        return every[HALF + step : HALF + step + owners, HALF - step]

    role = role[:, None]
    before, after = asked_from(-1), asked_from(1)
    even = role % 2 == 0
    union = asked_from(-2) | asked_from(2) | (even & before) | (~even & after)
    edge = ((role == 0) & before) | ((role == 3) & after)
    beside = (even & after) | (~even & before)
    return union, edge, beside


def body(source_field, weight_blocks, source_ids, target_ids):
    devices = lax.axis_size(AXES)
    n_gy = lax.axis_size("gy")
    me = lax.axis_index(AXES)
    held = weight_blocks.shape[0]
    nb = source_field.shape[0]
    blocks = jnp.arange(nb, dtype=jnp.int32)
    span = 2 * HALF
    ids = jnp.pad(source_ids.reshape(devices, held), ((span, span), (0, 0)), constant_values=-(2**20))
    window = lax.dynamic_slice_in_dim(ids, me, 2 * span + 1, 0)
    sender = me - span + jnp.arange(2 * span + 1, dtype=jnp.int32)[:, None]
    role = (me - HALF + QUAD + jnp.arange(SPAN, dtype=jnp.int32)) % QUAD
    union, edge, beside = wanted(named_blocks(window, sender, nb), role)
    rest = union & ~edge
    sets = jnp.stack([edge, rest, beside]).astype(jnp.bfloat16)
    earlier = (blocks[:, None] < blocks[None, :]).astype(jnp.bfloat16)
    ranks = jnp.einsum("sdb,bc->sdc", sets, earlier, preferred_element_type=jnp.float32).astype(jnp.int32)
    sizes = jnp.sum(sets.astype(jnp.float32), axis=2, keepdims=True).astype(jnp.int32)
    order = jnp.where(
        edge,
        ranks[0],
        jnp.where(rest, sizes[0] + ranks[1], sizes[0] + sizes[1] + blocks[None, :] - ranks[0] - ranks[1]),
    )
    aside = jnp.where(beside, ranks[2], nb)

    r = me % QUAD
    partner = HALF + 1 - 2 * (r % 2)
    mine = jnp.concatenate([aside[HALF : HALF + 1], order[HALF : HALF + 1]])
    chosen = jnp.sum(
        jnp.where(mine[:, None, :] == blocks[None, :, None], blocks[None, None, :], 0), axis=2
    )
    sel = jnp.concatenate([chosen[0, :CAP_S], chosen[1]])

    base_a, base_b, base_c, base_h, base_o = 0, nb, 2 * nb, 3 * nb, 3 * nb + CAP_S
    regions = jnp.array(
        [
            [base_b, base_c, base_o, base_h, base_a],
            [base_c, base_h, base_o, base_a, base_b],
            [base_b, base_a, base_o, base_h, base_c],
            [base_a, base_h, base_o, base_c, base_b],
        ],
        jnp.int32,
    )
    region = lax.dynamic_slice_in_dim(regions, r, 1, 0).reshape(SPAN, 1)
    from_partner = lax.dynamic_slice_in_dim(aside, partner, 1, 0)
    table = jnp.where(
        region == base_o, blocks[None, :], jnp.where(region == base_h, from_partner, order)
    )
    table = (region + table).reshape(-1)
    own_src = rows_of(source_ids, me, devices, held)
    low = (me - HALF) * nb
    hits = (own_src - low)[:, None] == jnp.arange(SPAN * nb, dtype=jnp.int32)[None, :]
    place = jnp.sum(jnp.where(hits, table[None, :], 0), axis=1)

    own_tgt = rows_of(target_ids, me, devices, held)
    low = (me - HALF) * TB_DEV
    tgt_asked = named(own_tgt, low, SPAN * TB_DEV).reshape(SPAN, TB_DEV)
    steps = jnp.arange(SPAN, dtype=jnp.int32)[:, None] - HALF
    tgt_group = HALF - jnp.abs(steps)
    tgt_slot = 1 + ranks_of(tgt_asked) + jnp.where(steps > 0, CAP_T, 0)
    hits = (own_tgt - low)[:, None] == jnp.arange(SPAN * TB_DEV, dtype=jnp.int32)[None, :]
    marks = jnp.sum(jnp.where(hits, (tgt_slot + 64 * tgt_group).reshape(-1)[None, :], 0), axis=1)
    group, slot = marks // 64, marks % 64

    index = jnp.arange(held, dtype=jnp.int32)
    groups = jnp.arange(4, dtype=jnp.int32)
    sizes = jnp.sum((group[None, :] == groups[:, None]).astype(jnp.int32), axis=1)
    sizes = (sizes + GROUP - 1) // GROUP * GROUP
    bounds = jnp.sum(jnp.where(groups[None, :] < groups[:, None], sizes[None, :], 0), axis=1)
    earlier = (group[:, None] == group[None, :]) & (index[:, None] < index[None, :])
    position = jnp.sum(earlier.astype(jnp.int32), axis=0)
    position = position + jnp.sum(
        jnp.where(group[None, :] == groups[:, None], bounds[:, None], 0), axis=0
    )
    item = (index * 1024 + place) * 64 + slot
    spots = jnp.arange(held + 4 * GROUP, dtype=jnp.int32)
    packed = jnp.sum(jnp.where(position[None, :] == spots[:, None], item[None, :], 0), axis=1)

    box_asked = []
    for step in range(-HALF, HALF + 1):
        sender = me - step
        valid = (sender >= 0) & (sender < devices)
        rows = rows_of(target_ids, sender, devices, held)
        box_asked.append(named(rows, me * TB_DEV, TB_DEV) & valid)
    box_asked = jnp.stack(box_asked)
    spot = jnp.where(box_asked, ranks_of(box_asked), -1)
    targets = jnp.sum(
        jnp.where(
            spot[:, None, :] == jnp.arange(CAP_T, dtype=jnp.int32)[None, :, None],
            1 + jnp.arange(TB_DEV, dtype=jnp.int32)[None, None, :],
            0,
        ),
        axis=2,
    ).reshape(-1)

    def finish(rare, bounds, packed, sel, targets, source_field, weight_blocks, source_ids):
        sel, bounds, packed, targets = lax.optimization_barrier((sel, bounds, packed, targets))
        pool = exchange_call(n_gy, devices, rare, sel, source_field)
        weights = weight_blocks
        boxes = [None] * SPAN
        below, above = products_call((0,), rare, held, bounds, packed, weights, pool)
        bounds, below, above = lax.optimization_barrier((bounds, below, above))
        boxes[0] = passed_along(below, -2)
        boxes[4] = passed_along(above, 2)
        below, above, own = products_call((1, 2), rare, held, bounds, packed, weights, pool)
        boxes[1] = passed_along(below, -1)
        boxes[3] = passed_along(above, 1)
        boxes[2], source_ids = lax.optimization_barrier((own, source_ids))
        return final_call(targets, boxes), source_ids

    arrays = (bounds, packed, sel, targets, source_field, weight_blocks, source_ids)
    result, late_ids = finish(False, *arrays)
    every = named_blocks(
        late_ids.reshape(devices, held), jnp.arange(devices, dtype=jnp.int32)[:, None], nb
    )
    every = jnp.pad(every, ((HALF, HALF), (0, 0), (0, 0)))
    union, _, _ = wanted(every, jnp.arange(devices, dtype=jnp.int32) % QUAD)
    most = jnp.max(jnp.sum(union.astype(jnp.int32), axis=1))
    return lax.cond(
        most > nb - RARE, lambda result, *arrays: finish(True, *arrays)[0], lambda result, *arrays: result, result, *arrays
    )


def solution(mesh):
    return jax.shard_map(
        body,
        mesh=mesh,
        in_specs=(P(AXES, None, None), P(AXES, None, None), P(), P()),
        out_specs=P(AXES, None, None),
        check_vma=False,
    )
```

profile of v0, /device:TPU:12, one launch (start us, length us, event | category | flops | bytes accessed | tf_op | source)
XLA Modules:
  0.0 291.0 jit_solution(3092064711905938257)
XLA Ops:
  0.0 0.7 fusion.41
  0.7 0.7 broadcast_compare_fusion.3
  1.5 0.9 reshape.832
  2.3 0.1 add_select_fusion.3
  2.4 1.2 fusion.5
  3.7 0.1 fusion.35
  3.8 0.1 fusion.34
  3.8 0.1 convert_reduce_fusion.4
  3.9 0.1 convolution_convert_fusion
  4.1 0.1 fusion.18
  4.2 0.1 select_reduce_fusion.3
  4.4 0.9 fusion.52
  5.2 0.2 compare_reduce_fusion
  5.5 0.1 and.518
  5.6 0.3 compare_reduce_fusion.1
  5.9 0.2 convert_reduce_fusion.1
  6.1 0.1 add_add_fusion
  6.2 0.1 add.417
  6.3 0.2 select_reduce_fusion.2
  6.4 0.1 fusion.25
  6.5 0.3 select_reduce_fusion
  6.8 0.1 convert_reduce_fusion.5
  6.9 0.2 convert_reduce_fusion
  7.1 0.2 select_reduce_fusion.4
  7.3 0.1 reshape.833.targets
  7.4 0.1 select_reduce_fusion.6.bounds
  7.5 0.1 select_reduce_fusion.5
  7.6 0.1 pad_add_fusion.2.sel
  7.7 0.2 select_reduce_fusion.1.packed
  7.9 0.0 copy-start.1
  7.9 180.7 %exchange.1.pool = bf16[576,128,128]{2,1,0:T(8,128)(2,1)S(1)} custom-call(s32[192]{0:T(256)S(1)} %pad_add_fusion.2.sel, bf16[128,128,128]{2,1,0:T(8,128)(2,1)} %src.1), custom_call_target="tpu_custom_call" | custom-call | flops 20000000000 | bytes 8388608 | tf_op jit(solution)/shard_map/exchange/pallas_call | solution.py:227
  188.6 0.0 copy-done.1
  188.7 8.2 %shard_map.57 = (s16[2064,128]{1,0:T(8,128)(2,1)}, s16[2064,128]{1,0:T(8,128)(2,1)}) custom-call(s32[4]{0:T(128)S(1)} %select_reduce_fusion.6.bounds, s32[544]{0:T(1024)S(1)} %select_reduce_fusion.1.packed, bf16[512,128,128]{2,1,0:T(8,128)(2,1)S(1)} %copy-done.1, bf16[576,128,128]{2,1,0:T(8,128)(2,1)S(1)} %exchange.1.pool), custom_call_target="tpu_custom_call" | custom-call | flops 713031680 | bytes 8388608 | tf_op jit(solution)/shard_map/pallas_call | solution.py:299
  196.9 0.0 copy-start.3
  196.9 14.0 %shard_map.58 = (s16[2064,128]{1,0:T(8,128)(2,1)}, s16[2064,128]{1,0:T(8,128)(2,1)}, f32[16,128,128]{2,1,0:T(8,128)S(1)}) custom-call(s32[4]{0:T(128)S(1)} %select_reduce_fusion.6.bounds, s32[544]{0:T(1024)S(1)} %select_reduce_fusion.1.packed, bf16[512,128,128]{2,1,0:T(8,128)(2,1)S(1)} %copy-done.1, bf16[576,128,128]{2,1,0:T(8,128)(2,1)S(1)} %exchange.1.pool), custom_call_target="tpu_custom_call" | custom-call | flops 1430257664 | bytes 8388608 | tf_op jit(solution)/shard_map/pallas_call | solution.py:299
  210.9 7.3 %collective-permute-start.5 = (s16[2064,128]{1,0:T(8,128)(2,1)}, s16[2064,128]{1,0:T(8,128)(2,1)S(1)}, u32[]{:S(2)}, u32[]{:S(2)}) collective-permute-start(s16[2064,128]{1,0:T(8,128)(2,1)} %get-tuple-element.64), channel_id=1, source_target_pairs={{1,0},{2,1},{3,2},{4,3},{5,4},{6,5},{7,6},{8,7},{9,8},{10,9},{11,1... | collective-permute-start | bytes 1585160 | tf_op jit(solution)/shard_map/ppermute | solution.py:29
  218.3 1.9 collective-permute-start.6
  220.2 9.8 %collective-permute-start.4 = (s16[2064,128]{1,0:T(8,128)(2,1)}, s16[2064,128]{1,0:T(8,128)(2,1)S(1)}, u32[]{:S(2)}, u32[]{:S(2)}) collective-permute-start(s16[2064,128]{1,0:T(8,128)(2,1)} %get-tuple-element.63), channel_id=1, source_target_pairs={{2,0},{3,1},{4,2},{5,3},{6,4},{7,5},{8,6},{9,7},{10,8},{11,9},{12,... | collective-permute-start | bytes 1585160 | tf_op jit(solution)/shard_map/ppermute | solution.py:29
  230.0 1.9 collective-permute-start.7
  231.9 0.0 copy-done.3
  232.0 0.1 add_select_fusion.1
  232.1 3.7 %fusion.4 = pred[32,5,128]{2,1,0:T(8,128)(4,1)S(1)} fusion(s32[32,512]{1,0:T(8,128)S(1)} %get-tuple-element.86, s32[32,512]{1,0:T(8,128)S(1)} %get-tuple-element.85), kind=kOutput, calls=%fused_computation.8 | convolution fusion | flops 23171072 | bytes 151552 | tf_op jit(solution)/shard_map/dot_general | solution.py:361
  235.8 0.1 fusion.9
  235.9 0.2 convert_reduce_fusion.3
  236.1 0.7 reduce_max.9
  237.4 5.3 %collective-permute-done.5.refs_1_ = s16[2064,128]{1,0:T(8,128)(2,1)S(1)} collective-permute-done((s16[2064,128]{1,0:T(8,128)(2,1)}, s16[2064,128]{1,0:T(8,128)(2,1)S(1)}, u32[]{:S(2)}, u32[]{:S(2)}) %collective-permute-start.5) | collective-permute-done | bytes 528416 | tf_op jit(solution)/shard_map/ppermute | solution.py:29
  242.7 3.9 %collective-permute-done.6.refs_3_ = s16[2064,128]{1,0:T(8,128)(2,1)S(1)} collective-permute-done((s16[2064,128]{1,0:T(8,128)(2,1)}, s16[2064,128]{1,0:T(8,128)(2,1)S(1)}, u32[]{:S(2)}, u32[]{:S(2)}) %collective-permute-start.6) | collective-permute-done | bytes 528416 | tf_op jit(solution)/shard_map/ppermute | solution.py:29
  246.7 30.0 %collective-permute-done.4.refs_0_ = s16[2064,128]{1,0:T(8,128)(2,1)S(1)} collective-permute-done((s16[2064,128]{1,0:T(8,128)(2,1)}, s16[2064,128]{1,0:T(8,128)(2,1)S(1)}, u32[]{:S(2)}, u32[]{:S(2)}) %collective-permute-start.4) | collective-permute-done | bytes 528416 | tf_op jit(solution)/shard_map/ppermute | solution.py:29
  276.7 10.6 %collective-permute-done.7.refs_4_ = s16[2064,128]{1,0:T(8,128)(2,1)} collective-permute-done((s16[2064,128]{1,0:T(8,128)(2,1)}, s16[2064,128]{1,0:T(8,128)(2,1)}, u32[]{:S(2)}, u32[]{:S(2)}) %collective-permute-start.7) | collective-permute-done | bytes 528416 | tf_op jit(solution)/shard_map/ppermute | solution.py:29
  287.3 2.3 final_sum.3
  289.7 0.0 copy-start.2
  289.7 1.3 copy-done.2
  (31 shorter events, 0.3 us)
Async XLA Ops:
  7.9 180.7 %copy-start.1 = (bf16[512,128,128]{2,1,0:T(8,128)(2,1)S(1)}, bf16[512,128,128]{2,1,0:T(8,128)(2,1)}, u32[]{:S(2)}) copy-start(bf16[512,128,128]{2,1,0:T(8,128)(2,1)} %weights.3) | copy-start | bytes 50331652
  196.9 35.0 %copy-start.3 = (s32[16384]{0:T(1024)S(1)}, s32[16384]{0:T(1024)}, u32[]{:S(2)}) copy-start(s32[16384]{0:T(1024)} %param.9) | copy-start | bytes 196612
  210.9 31.8 %collective-permute-start.5 = (s16[2064,128]{1,0:T(8,128)(2,1)}, s16[2064,128]{1,0:T(8,128)(2,1)S(1)}, u32[]{:S(2)}, u32[]{:S(2)}) collective-permute-start(s16[2064,128]{1,0:T(8,128)(2,1)} %get-tuple-element.64), channel_id=1, source_target_pairs={{1,0},{2,1},{3,2},{4,3},{5,4},{6,5},{7,6},{8,7},{9,8},{10,9},{11,1... | collective-permute-start | bytes 1585160 | tf_op jit(solution)/shard_map/ppermute | solution.py:29
  218.3 28.4 %collective-permute-start.6 = (s16[2064,128]{1,0:T(8,128)(2,1)}, s16[2064,128]{1,0:T(8,128)(2,1)S(1)}, u32[]{:S(2)}, u32[]{:S(2)}) collective-permute-start(s16[2064,128]{1,0:T(8,128)(2,1)} %get-tuple-element.66), channel_id=1, source_target_pairs={{0,1},{1,2},{2,3},{3,4},{4,5},{5,6},{6,7},{7,8},{8,9},{9,10},{10,1... | collective-permute-start | bytes 1585160 | tf_op jit(solution)/shard_map/ppermute | solution.py:29
  220.2 56.5 %collective-permute-start.4 = (s16[2064,128]{1,0:T(8,128)(2,1)}, s16[2064,128]{1,0:T(8,128)(2,1)S(1)}, u32[]{:S(2)}, u32[]{:S(2)}) collective-permute-start(s16[2064,128]{1,0:T(8,128)(2,1)} %get-tuple-element.63), channel_id=1, source_target_pairs={{2,0},{3,1},{4,2},{5,3},{6,4},{7,5},{8,6},{9,7},{10,8},{11,9},{12,... | collective-permute-start | bytes 1585160 | tf_op jit(solution)/shard_map/ppermute | solution.py:29
  230.0 57.3 %collective-permute-start.7 = (s16[2064,128]{1,0:T(8,128)(2,1)}, s16[2064,128]{1,0:T(8,128)(2,1)}, u32[]{:S(2)}, u32[]{:S(2)}) collective-permute-start(s16[2064,128]{1,0:T(8,128)(2,1)} %get-tuple-element.67), channel_id=1, source_target_pairs={{0,2},{1,3},{2,4},{3,5},{4,6},{5,7},{6,8},{7,9},{8,10},{9,11},{10,... | collective-permute-start | bytes 1585160 | tf_op jit(solution)/shard_map/ppermute | solution.py:29
  289.7 1.3 copy-start.2
where the time goes:
time: 292 us; the launch traced here: 291 us
  Pallas kernels  205 us (70%)
  waiting for transfers between devices  49.9 us (17%)
  starting transfers between devices  21 us (7%)
  other arithmetic  5.65 us (2%)
  matrix products  5.05 us (2%)
  local copies, waits for them, and re-layouts  3.17 us (1%)
    pallas_call x1, Pallas kernels, exchange_call(): pl.pallas_call(functools.partial(exchange_kernel, devices, n_gy, count),...  181 us
    ppermute x4, waiting for transfers between devices, passed_along(): lax.ppermute(value, AXES, [(source, source + steps) for source in range(i...  49.9 us
    pallas_call x2, Pallas kernels, products_call(): pl.pallas_call(functools.partial(products_kernel, groups), out_shape=out_...  22.3 us
    ppermute x4, starting transfers between devices, passed_along(): lax.ppermute(value, AXES, [(source, source + steps) for source in range(i...  21 us
  transfers between devices with their start and end apart: 4, of which 4 were waited for; matrix products, arithmetic and copies ran while one was open for 2% of the time, Pallas kernels for 0%

commit v1 on v0

--- a/solution.py
+++ b/solution.py
@@ -17,7 +17,7 @@
 MESH = pl.DeviceIdType.MESH
 QUAD = 4
 CHUNK = 4
-GROUP = 8
+GROUP = 32
 TILE = 128
 RARE = 12
 LOW_EXPONENT = -110.0
@@ -375,7 +375,7 @@
 
     role = role[:, None]
     before, after = asked_from(-1), asked_from(1)
-    even = role % 2 == 0
+    even = (role & 1) == 0
     union = asked_from(-2) | asked_from(2) | (even & before) | (~even & after)
     edge = ((role == 0) & before) | ((role == 3) & after)
     beside = (even & after) | (~even & before)
@@ -390,10 +390,11 @@
     nb = source_field.shape[0]
     blocks = jnp.arange(nb, dtype=jnp.int32)
     span = 2 * HALF
-    ids = jnp.pad(source_ids.reshape(devices, held), ((span, span), (0, 0)), constant_values=-(2**20))
-    window = lax.dynamic_slice_in_dim(ids, me, 2 * span + 1, 0)
+    ids = jnp.pad(source_ids, (span * held, span * held), constant_values=-(2**20))
+    window = lax.dynamic_slice_in_dim(ids, me * held, (2 * span + 1) * held, 0)
+    window = window.reshape(2 * span + 1, held)
     sender = me - span + jnp.arange(2 * span + 1, dtype=jnp.int32)[:, None]
-    role = (me - HALF + QUAD + jnp.arange(SPAN, dtype=jnp.int32)) % QUAD
+    role = (me - HALF + jnp.arange(SPAN, dtype=jnp.int32)) & (QUAD - 1)
     union, edge, beside = wanted(named_blocks(window, sender, nb), role)
     rest = union & ~edge
     sets = jnp.stack([edge, rest, beside]).astype(jnp.bfloat16)
@@ -407,8 +408,8 @@
     )
     aside = jnp.where(beside, ranks[2], nb)
 
-    r = me % QUAD
-    partner = HALF + 1 - 2 * (r % 2)
+    r = me & (QUAD - 1)
+    partner = HALF + 1 - 2 * (r & 1)
     mine = jnp.concatenate([aside[HALF : HALF + 1], order[HALF : HALF + 1]])
     chosen = jnp.sum(
         jnp.where(mine[:, None, :] == blocks[None, :, None], blocks[None, None, :], 0), axis=2

time: 292 us -> 285 us (0.976)
  Pallas kernels: 205 us -> 198 us
    pallas_call x2, Pallas kernels: 22.3 us -> 15.1 us  [products_call(): pl.pallas_call(functools.partial(products_kernel, groups), out_shape=out_...]
where the time goes in v1:
time: 285 us; the launch traced here: 284 us
  Pallas kernels  198 us (69%)
  waiting for transfers between devices  49.8 us (17%)
  starting transfers between devices  21.2 us (7%)
  other arithmetic  5.63 us (2%)
  matrix products  5.05 us (2%)
  local copies, waits for them, and re-layouts  3.16 us (1%)
    pallas_call x1, Pallas kernels, exchange_call(): pl.pallas_call(functools.partial(exchange_kernel, devices, n_gy, count),...  181 us
    ppermute x4, waiting for transfers between devices, passed_along(): lax.ppermute(value, AXES, [(source, source + steps) for source in range(i...  49.8 us
    ppermute x4, starting transfers between devices, passed_along(): lax.ppermute(value, AXES, [(source, source + steps) for source in range(i...  21.2 us
    pallas_call x2, Pallas kernels, products_call(): pl.pallas_call(functools.partial(products_kernel, groups), out_shape=out_...  15.1 us
  transfers between devices with their start and end apart: 4, of which 4 were waited for; matrix products, arithmetic and copies ran while one was open for 2% of the time, Pallas kernels for 0%

profile of v1, /device:TPU:12, one launch (start us, length us, event | category | flops | bytes accessed | tf_op | source)
XLA Modules:
  0.0 283.9 jit_solution(3696074417233734759)
XLA Ops:
  0.0 0.7 dynamic-slice_bitcast_fusion.1
  0.7 0.7 broadcast_compare_fusion.2
  1.5 0.8 pad_dynamic-slice_fusion
  2.3 0.1 add_select_fusion.3
  2.4 1.2 fusion.5
  3.6 0.1 fusion.35
  3.7 0.1 fusion.34
  3.8 0.1 convert_reduce_fusion.4
  3.9 0.1 convolution_convert_fusion
  4.0 0.1 fusion.18
  4.2 0.1 select_reduce_fusion.3
  4.3 0.9 fusion.47
  5.2 0.2 compare_reduce_fusion
  5.4 0.1 and.508
  5.5 0.3 compare_reduce_fusion.1
  5.9 0.2 convert_reduce_fusion.1
  6.1 0.1 add_add_fusion
  6.1 0.1 add.361
  6.2 0.2 select_reduce_fusion.2
  6.4 0.1 fusion.25
  6.5 0.3 select_reduce_fusion.1
  6.8 0.1 convert_reduce_fusion.5
  6.9 0.2 convert_reduce_fusion
  7.1 0.2 select_reduce_fusion.4
  7.3 0.1 reshape.852.targets
  7.4 0.1 select_reduce_fusion.6.bounds
  7.5 0.1 select_reduce_fusion.5
  7.6 0.1 pad_add_fusion.2.sel
  7.6 0.2 select_reduce_fusion.packed
  7.9 0.0 copy-start.1
  7.9 180.7 %exchange.1.pool = bf16[576,128,128]{2,1,0:T(8,128)(2,1)S(1)} custom-call(s32[192]{0:T(256)S(1)} %pad_add_fusion.2.sel, bf16[128,128,128]{2,1,0:T(8,128)(2,1)} %src.1), custom_call_target="tpu_custom_call" | custom-call | flops 20000000000 | bytes 8388608 | tf_op jit(solution)/shard_map/exchange/pallas_call | solution.py:227
  188.6 0.0 copy-done.1
  188.6 6.2 %shard_map.57 = (s16[2064,128]{1,0:T(8,128)(2,1)}, s16[2064,128]{1,0:T(8,128)(2,1)}) custom-call(s32[4]{0:T(128)S(1)} %select_reduce_fusion.6.bounds, s32[640]{0:T(1024)S(1)} %select_reduce_fusion.packed, bf16[512,128,128]{2,1,0:T(8,128)(2,1)S(1)} %copy-done.1, bf16[576,128,128]{2,1,0:T(8,128)(2,1)S(1)} %exchange.1.pool), custom_call_target="tpu_custom_call" | custom-call | flops 713031680 | bytes 8388608 | tf_op jit(solution)/shard_map/pallas_call | solution.py:299
  194.8 0.0 copy-start.3
  194.8 8.9 %shard_map.58 = (s16[2064,128]{1,0:T(8,128)(2,1)}, s16[2064,128]{1,0:T(8,128)(2,1)}, f32[16,128,128]{2,1,0:T(8,128)S(1)}) custom-call(s32[4]{0:T(128)S(1)} %select_reduce_fusion.6.bounds, s32[640]{0:T(1024)S(1)} %select_reduce_fusion.packed, bf16[512,128,128]{2,1,0:T(8,128)(2,1)S(1)} %copy-done.1, bf16[576,128,128]{2,1,0:T(8,128)(2,1)S(1)} %exchange.1.pool), custom_call_target="tpu_custom_call" | custom-call | flops 1430257664 | bytes 8388608 | tf_op jit(solution)/shard_map/pallas_call | solution.py:299
  203.7 7.6 %collective-permute-start.5 = (s16[2064,128]{1,0:T(8,128)(2,1)}, s16[2064,128]{1,0:T(8,128)(2,1)S(1)}, u32[]{:S(2)}, u32[]{:S(2)}) collective-permute-start(s16[2064,128]{1,0:T(8,128)(2,1)} %get-tuple-element.64), channel_id=1, source_target_pairs={{1,0},{2,1},{3,2},{4,3},{5,4},{6,5},{7,6},{8,7},{9,8},{10,9},{11,1... | collective-permute-start | bytes 1585160 | tf_op jit(solution)/shard_map/ppermute | solution.py:29
  211.3 1.9 collective-permute-start.6
  213.2 9.8 %collective-permute-start.4 = (s16[2064,128]{1,0:T(8,128)(2,1)}, s16[2064,128]{1,0:T(8,128)(2,1)S(1)}, u32[]{:S(2)}, u32[]{:S(2)}) collective-permute-start(s16[2064,128]{1,0:T(8,128)(2,1)} %get-tuple-element.63), channel_id=1, source_target_pairs={{2,0},{3,1},{4,2},{5,3},{6,4},{7,5},{8,6},{9,7},{10,8},{11,9},{12,... | collective-permute-start | bytes 1585160 | tf_op jit(solution)/shard_map/ppermute | solution.py:29
  223.0 1.9 collective-permute-start.7
  225.0 0.0 copy-done.3
  225.0 0.1 add_select_fusion.1
  225.2 3.7 %fusion.4 = pred[32,5,128]{2,1,0:T(8,128)(4,1)S(1)} fusion(s32[32,512]{1,0:T(8,128)S(1)} %get-tuple-element.86, s32[32,512]{1,0:T(8,128)S(1)} %get-tuple-element.85), kind=kOutput, calls=%fused_computation.10 | convolution fusion | flops 23171072 | bytes 151552 | tf_op jit(solution)/shard_map/dot_general | solution.py:361
  228.9 0.1 fusion.9
  228.9 0.2 convert_reduce_fusion.3
  229.1 0.7 reduce_max.9
  230.4 5.3 %collective-permute-done.5.refs_1_ = s16[2064,128]{1,0:T(8,128)(2,1)S(1)} collective-permute-done((s16[2064,128]{1,0:T(8,128)(2,1)}, s16[2064,128]{1,0:T(8,128)(2,1)S(1)}, u32[]{:S(2)}, u32[]{:S(2)}) %collective-permute-start.5) | collective-permute-done | bytes 528416 | tf_op jit(solution)/shard_map/ppermute | solution.py:29
  235.7 4.0 %collective-permute-done.6.refs_3_ = s16[2064,128]{1,0:T(8,128)(2,1)S(1)} collective-permute-done((s16[2064,128]{1,0:T(8,128)(2,1)}, s16[2064,128]{1,0:T(8,128)(2,1)S(1)}, u32[]{:S(2)}, u32[]{:S(2)}) %collective-permute-start.6) | collective-permute-done | bytes 528416 | tf_op jit(solution)/shard_map/ppermute | solution.py:29
  239.7 29.7 %collective-permute-done.4.refs_0_ = s16[2064,128]{1,0:T(8,128)(2,1)S(1)} collective-permute-done((s16[2064,128]{1,0:T(8,128)(2,1)}, s16[2064,128]{1,0:T(8,128)(2,1)S(1)}, u32[]{:S(2)}, u32[]{:S(2)}) %collective-permute-start.4) | collective-permute-done | bytes 528416 | tf_op jit(solution)/shard_map/ppermute | solution.py:29
  269.4 10.8 %collective-permute-done.7.refs_4_ = s16[2064,128]{1,0:T(8,128)(2,1)} collective-permute-done((s16[2064,128]{1,0:T(8,128)(2,1)}, s16[2064,128]{1,0:T(8,128)(2,1)}, u32[]{:S(2)}, u32[]{:S(2)}) %collective-permute-start.7) | collective-permute-done | bytes 528416 | tf_op jit(solution)/shard_map/ppermute | solution.py:29
  280.3 2.3 final_sum.3
  282.6 0.0 copy-start.2
  282.6 1.3 copy-done.2
  (32 shorter events, 0.3 us)
Async XLA Ops:
  7.9 180.7 %copy-start.1 = (bf16[512,128,128]{2,1,0:T(8,128)(2,1)S(1)}, bf16[512,128,128]{2,1,0:T(8,128)(2,1)}, u32[]{:S(2)}) copy-start(bf16[512,128,128]{2,1,0:T(8,128)(2,1)} %weights.3) | copy-start | bytes 50331652
  194.8 30.2 %copy-start.3 = (s32[16384]{0:T(1024)S(1)}, s32[16384]{0:T(1024)}, u32[]{:S(2)}) copy-start(s32[16384]{0:T(1024)} %param.9) | copy-start | bytes 196612
  203.7 32.0 %collective-permute-start.5 = (s16[2064,128]{1,0:T(8,128)(2,1)}, s16[2064,128]{1,0:T(8,128)(2,1)S(1)}, u32[]{:S(2)}, u32[]{:S(2)}) collective-permute-start(s16[2064,128]{1,0:T(8,128)(2,1)} %get-tuple-element.64), channel_id=1, source_target_pairs={{1,0},{2,1},{3,2},{4,3},{5,4},{6,5},{7,6},{8,7},{9,8},{10,9},{11,1... | collective-permute-start | bytes 1585160 | tf_op jit(solution)/shard_map/ppermute | solution.py:29
  211.3 28.4 %collective-permute-start.6 = (s16[2064,128]{1,0:T(8,128)(2,1)}, s16[2064,128]{1,0:T(8,128)(2,1)S(1)}, u32[]{:S(2)}, u32[]{:S(2)}) collective-permute-start(s16[2064,128]{1,0:T(8,128)(2,1)} %get-tuple-element.66), channel_id=1, source_target_pairs={{0,1},{1,2},{2,3},{3,4},{4,5},{5,6},{6,7},{7,8},{8,9},{9,10},{10,1... | collective-permute-start | bytes 1585160 | tf_op jit(solution)/shard_map/ppermute | solution.py:29
  213.2 56.2 %collective-permute-start.4 = (s16[2064,128]{1,0:T(8,128)(2,1)}, s16[2064,128]{1,0:T(8,128)(2,1)S(1)}, u32[]{:S(2)}, u32[]{:S(2)}) collective-permute-start(s16[2064,128]{1,0:T(8,128)(2,1)} %get-tuple-element.63), channel_id=1, source_target_pairs={{2,0},{3,1},{4,2},{5,3},{6,4},{7,5},{8,6},{9,7},{10,8},{11,9},{12,... | collective-permute-start | bytes 1585160 | tf_op jit(solution)/shard_map/ppermute | solution.py:29
  223.0 57.2 %collective-permute-start.7 = (s16[2064,128]{1,0:T(8,128)(2,1)}, s16[2064,128]{1,0:T(8,128)(2,1)}, u32[]{:S(2)}, u32[]{:S(2)}) collective-permute-start(s16[2064,128]{1,0:T(8,128)(2,1)} %get-tuple-element.67), channel_id=1, source_target_pairs={{0,2},{1,3},{2,4},{3,5},{4,6},{5,7},{6,8},{7,9},{8,10},{9,11},{10,... | collective-permute-start | bytes 1585160 | tf_op jit(solution)/shard_map/ppermute | solution.py:29
  282.6 1.3 copy-start.2

commit v2 on v1

--- a/solution.py
+++ b/solution.py
@@ -18,6 +18,7 @@
 QUAD = 4
 CHUNK = 4
 GROUP = 32
+CLOSE = 8
 TILE = 128
 RARE = 12
 LOW_EXPONENT = -110.0
@@ -75,8 +76,6 @@
     pl.when(inner)(lambda: greet(near))
     pl.when(has_to)(lambda: greet(to))
     pl.when(has_from)(lambda: greet(source))
-    peers = 2 + inner.astype(jnp.int32) + has_to.astype(jnp.int32) + has_from.astype(jnp.int32)
-    pl.semaphore_wait(barrier, peers)
 
     def piece(base, k):
         return recv.at[pl.ds(base + k * CHUNK, CHUNK)]
@@ -132,6 +131,9 @@
 
     lax.fori_loop(0, pieces, pick, 0)
     lax.fori_loop(0, half, pick_side, 0)
+
+    peers = 2 + inner.astype(jnp.int32) + has_to.astype(jnp.int32) + has_from.astype(jnp.int32)
+    pl.semaphore_wait(barrier, peers)
 
     @pl.when(inner)
     def _():
@@ -329,11 +331,11 @@
     lax.fori_loop(0, CAP_T, one, 0)
 
     def close(g, carry):
-        for u in range(GROUP):
-            out[g * GROUP + u] = acc[1 + g * GROUP + u].astype(out.dtype)
+        for u in range(CLOSE):
+            out[g * CLOSE + u] = acc[1 + g * CLOSE + u].astype(out.dtype)
         return carry
 
-    lax.fori_loop(0, TB_DEV // GROUP, close, 0)
+    lax.fori_loop(0, TB_DEV // CLOSE, close, 0)
 
 
 def final_call(targets, boxes):

time: 285 us -> 282 us (0.989)
  Pallas kernels: 198 us -> 195 us
where the time goes in v2:
time: 282 us; the launch traced here: 281 us
  Pallas kernels  195 us (69%)
  waiting for transfers between devices  49.3 us (17%)
  starting transfers between devices  21.7 us (8%)
  other arithmetic  5.63 us (2%)
  matrix products  5.05 us (2%)
  local copies, waits for them, and re-layouts  3.16 us (1%)
    pallas_call x1, Pallas kernels, exchange_call(): pl.pallas_call(functools.partial(exchange_kernel, devices, n_gy, count),...  178 us
    ppermute x4, waiting for transfers between devices, passed_along(): lax.ppermute(value, AXES, [(source, source + steps) for source in range(i...  49.3 us
    ppermute x4, starting transfers between devices, passed_along(): lax.ppermute(value, AXES, [(source, source + steps) for source in range(i...  21.7 us
    pallas_call x2, Pallas kernels, products_call(): pl.pallas_call(functools.partial(products_kernel, groups), out_shape=out_...  15.1 us
  transfers between devices with their start and end apart: 4, of which 4 were waited for; matrix products, arithmetic and copies ran while one was open for 2% of the time, Pallas kernels for 0%

profile of v2, /device:TPU:12, one launch (start us, length us, event | category | flops | bytes accessed | tf_op | source)
XLA Modules:
  0.0 281.2 jit_solution(1221944373128521390)
XLA Ops:
  0.0 0.7 dynamic-slice_bitcast_fusion.1
  0.7 0.7 broadcast_compare_fusion.2
  1.5 0.8 pad_dynamic-slice_fusion
  2.3 0.1 add_select_fusion.3
  2.4 1.2 fusion.5
  3.6 0.1 fusion.35
  3.7 0.1 fusion.34
  3.8 0.1 convert_reduce_fusion.4
  3.9 0.1 convolution_convert_fusion
  4.0 0.1 fusion.18
  4.2 0.1 select_reduce_fusion.3
  4.3 0.9 fusion.47
  5.2 0.2 compare_reduce_fusion
  5.4 0.1 and.508
  5.5 0.3 compare_reduce_fusion.1
  5.9 0.2 convert_reduce_fusion.1
  6.1 0.1 add_add_fusion
  6.1 0.1 add.361
  6.2 0.2 select_reduce_fusion.2
  6.4 0.1 fusion.25
  6.5 0.3 select_reduce_fusion.1
  6.8 0.1 convert_reduce_fusion.5
  6.9 0.2 convert_reduce_fusion
  7.1 0.2 select_reduce_fusion.4
  7.3 0.1 reshape.852.targets
  7.4 0.1 select_reduce_fusion.6.bounds
  7.5 0.1 select_reduce_fusion.5
  7.6 0.1 pad_add_fusion.2.sel
  7.6 0.2 select_reduce_fusion.packed
  7.9 0.0 copy-start.1
  7.9 178.0 %exchange.1.pool = bf16[576,128,128]{2,1,0:T(8,128)(2,1)S(1)} custom-call(s32[192]{0:T(256)S(1)} %pad_add_fusion.2.sel, bf16[128,128,128]{2,1,0:T(8,128)(2,1)} %src.1), custom_call_target="tpu_custom_call" | custom-call | flops 20000000000 | bytes 8388608 | tf_op jit(solution)/shard_map/exchange/pallas_call | solution.py:229
  185.9 0.0 copy-done.1
  185.9 6.2 %shard_map.57 = (s16[2064,128]{1,0:T(8,128)(2,1)}, s16[2064,128]{1,0:T(8,128)(2,1)}) custom-call(s32[4]{0:T(128)S(1)} %select_reduce_fusion.6.bounds, s32[640]{0:T(1024)S(1)} %select_reduce_fusion.packed, bf16[512,128,128]{2,1,0:T(8,128)(2,1)S(1)} %copy-done.1, bf16[576,128,128]{2,1,0:T(8,128)(2,1)S(1)} %exchange.1.pool), custom_call_target="tpu_custom_call" | custom-call | flops 713031680 | bytes 8388608 | tf_op jit(solution)/shard_map/pallas_call | solution.py:301
  192.0 0.0 copy-start.3
  192.0 8.9 %shard_map.58 = (s16[2064,128]{1,0:T(8,128)(2,1)}, s16[2064,128]{1,0:T(8,128)(2,1)}, f32[16,128,128]{2,1,0:T(8,128)S(1)}) custom-call(s32[4]{0:T(128)S(1)} %select_reduce_fusion.6.bounds, s32[640]{0:T(1024)S(1)} %select_reduce_fusion.packed, bf16[512,128,128]{2,1,0:T(8,128)(2,1)S(1)} %copy-done.1, bf16[576,128,128]{2,1,0:T(8,128)(2,1)S(1)} %exchange.1.pool), custom_call_target="tpu_custom_call" | custom-call | flops 1430257664 | bytes 8388608 | tf_op jit(solution)/shard_map/pallas_call | solution.py:301
  201.0 7.9 %collective-permute-start.5 = (s16[2064,128]{1,0:T(8,128)(2,1)}, s16[2064,128]{1,0:T(8,128)(2,1)S(1)}, u32[]{:S(2)}, u32[]{:S(2)}) collective-permute-start(s16[2064,128]{1,0:T(8,128)(2,1)} %get-tuple-element.64), channel_id=1, source_target_pairs={{1,0},{2,1},{3,2},{4,3},{5,4},{6,5},{7,6},{8,7},{9,8},{10,9},{11,1... | collective-permute-start | bytes 1585160 | tf_op jit(solution)/shard_map/ppermute | solution.py:30
  208.8 1.9 collective-permute-start.6
  210.8 10.0 %collective-permute-start.4 = (s16[2064,128]{1,0:T(8,128)(2,1)}, s16[2064,128]{1,0:T(8,128)(2,1)S(1)}, u32[]{:S(2)}, u32[]{:S(2)}) collective-permute-start(s16[2064,128]{1,0:T(8,128)(2,1)} %get-tuple-element.63), channel_id=1, source_target_pairs={{2,0},{3,1},{4,2},{5,3},{6,4},{7,5},{8,6},{9,7},{10,8},{11,9},{12,... | collective-permute-start | bytes 1585160 | tf_op jit(solution)/shard_map/ppermute | solution.py:30
  220.8 1.9 collective-permute-start.7
  222.7 0.0 copy-done.3
  222.8 0.1 add_select_fusion.1
  222.9 3.7 %fusion.4 = pred[32,5,128]{2,1,0:T(8,128)(4,1)S(1)} fusion(s32[32,512]{1,0:T(8,128)S(1)} %get-tuple-element.86, s32[32,512]{1,0:T(8,128)S(1)} %get-tuple-element.85), kind=kOutput, calls=%fused_computation.10 | convolution fusion | flops 23171072 | bytes 151552 | tf_op jit(solution)/shard_map/dot_general | solution.py:363
  226.6 0.1 fusion.9
  226.7 0.2 convert_reduce_fusion.3
  226.9 0.7 reduce_max.9
  228.2 4.8 %collective-permute-done.5.refs_1_ = s16[2064,128]{1,0:T(8,128)(2,1)S(1)} collective-permute-done((s16[2064,128]{1,0:T(8,128)(2,1)}, s16[2064,128]{1,0:T(8,128)(2,1)S(1)}, u32[]{:S(2)}, u32[]{:S(2)}) %collective-permute-start.5) | collective-permute-done | bytes 528416 | tf_op jit(solution)/shard_map/ppermute | solution.py:30
  233.0 4.5 %collective-permute-done.6.refs_3_ = s16[2064,128]{1,0:T(8,128)(2,1)S(1)} collective-permute-done((s16[2064,128]{1,0:T(8,128)(2,1)}, s16[2064,128]{1,0:T(8,128)(2,1)S(1)}, u32[]{:S(2)}, u32[]{:S(2)}) %collective-permute-start.6) | collective-permute-done | bytes 528416 | tf_op jit(solution)/shard_map/ppermute | solution.py:30
  237.5 29.8 %collective-permute-done.4.refs_0_ = s16[2064,128]{1,0:T(8,128)(2,1)S(1)} collective-permute-done((s16[2064,128]{1,0:T(8,128)(2,1)}, s16[2064,128]{1,0:T(8,128)(2,1)S(1)}, u32[]{:S(2)}, u32[]{:S(2)}) %collective-permute-start.4) | collective-permute-done | bytes 528416 | tf_op jit(solution)/shard_map/ppermute | solution.py:30
  267.2 10.3 %collective-permute-done.7.refs_4_ = s16[2064,128]{1,0:T(8,128)(2,1)} collective-permute-done((s16[2064,128]{1,0:T(8,128)(2,1)}, s16[2064,128]{1,0:T(8,128)(2,1)}, u32[]{:S(2)}, u32[]{:S(2)}) %collective-permute-start.7) | collective-permute-done | bytes 528416 | tf_op jit(solution)/shard_map/ppermute | solution.py:30
  277.5 2.3 final_sum.3
  279.9 0.0 copy-start.2
  279.9 1.3 copy-done.2
  (32 shorter events, 0.3 us)
Async XLA Ops:
  7.9 178.0 %copy-start.1 = (bf16[512,128,128]{2,1,0:T(8,128)(2,1)S(1)}, bf16[512,128,128]{2,1,0:T(8,128)(2,1)}, u32[]{:S(2)}) copy-start(bf16[512,128,128]{2,1,0:T(8,128)(2,1)} %weights.3) | copy-start | bytes 50331652
  192.0 30.7 %copy-start.3 = (s32[16384]{0:T(1024)S(1)}, s32[16384]{0:T(1024)}, u32[]{:S(2)}) copy-start(s32[16384]{0:T(1024)} %param.9) | copy-start | bytes 196612
  201.0 32.0 %collective-permute-start.5 = (s16[2064,128]{1,0:T(8,128)(2,1)}, s16[2064,128]{1,0:T(8,128)(2,1)S(1)}, u32[]{:S(2)}, u32[]{:S(2)}) collective-permute-start(s16[2064,128]{1,0:T(8,128)(2,1)} %get-tuple-element.64), channel_id=1, source_target_pairs={{1,0},{2,1},{3,2},{4,3},{5,4},{6,5},{7,6},{8,7},{9,8},{10,9},{11,1... | collective-permute-start | bytes 1585160 | tf_op jit(solution)/shard_map/ppermute | solution.py:30
  208.8 28.6 %collective-permute-start.6 = (s16[2064,128]{1,0:T(8,128)(2,1)}, s16[2064,128]{1,0:T(8,128)(2,1)S(1)}, u32[]{:S(2)}, u32[]{:S(2)}) collective-permute-start(s16[2064,128]{1,0:T(8,128)(2,1)} %get-tuple-element.66), channel_id=1, source_target_pairs={{0,1},{1,2},{2,3},{3,4},{4,5},{5,6},{6,7},{7,8},{8,9},{9,10},{10,1... | collective-permute-start | bytes 1585160 | tf_op jit(solution)/shard_map/ppermute | solution.py:30
  210.8 56.5 %collective-permute-start.4 = (s16[2064,128]{1,0:T(8,128)(2,1)}, s16[2064,128]{1,0:T(8,128)(2,1)S(1)}, u32[]{:S(2)}, u32[]{:S(2)}) collective-permute-start(s16[2064,128]{1,0:T(8,128)(2,1)} %get-tuple-element.63), channel_id=1, source_target_pairs={{2,0},{3,1},{4,2},{5,3},{6,4},{7,5},{8,6},{9,7},{10,8},{11,9},{12,... | collective-permute-start | bytes 1585160 | tf_op jit(solution)/shard_map/ppermute | solution.py:30
  220.8 56.7 %collective-permute-start.7 = (s16[2064,128]{1,0:T(8,128)(2,1)}, s16[2064,128]{1,0:T(8,128)(2,1)}, u32[]{:S(2)}, u32[]{:S(2)}) collective-permute-start(s16[2064,128]{1,0:T(8,128)(2,1)} %get-tuple-element.67), channel_id=1, source_target_pairs={{0,2},{1,3},{2,4},{3,5},{4,6},{5,7},{6,8},{7,9},{8,10},{9,11},{10,... | collective-permute-start | bytes 1585160 | tf_op jit(solution)/shard_map/ppermute | solution.py:30
  279.9 1.3 copy-start.2
